TPU v7x, 16 devices: a whole 2x2x2 slice. The times are simulated.
16 devices in a mesh: data: 16 (over z, y, x, core).
Axes of the slice: x: 2, y: 2, z: 2, core: 2. Of those that a mesh axis runs over, the one named last changes fastest.
Arguments:
- x_in: bfloat16 [32, 1024, 1024], P('data')
- dy_out: bfloat16 [32, 1024, 1024], P('data')
- lengths: int32 [32], P('data')
- w_one: bfloat16 [4, 1024, 4096], replicated
- w_two: bfloat16 [4, 4096, 1024], replicated
- noise_one: float32 [4, 1024, 4096], replicated
- noise_two: float32 [4, 4096, 1024], replicated
- clip_norm: float32 [1], replicated
Outputs:
- output 1: float32 [4, 1024, 4096], replicated
- output 2: float32 [4, 4096, 1024], replicated
All inputs are finite; a program needn't handle non-finite values.
Results may differ from a plain program's by a relative error of at most 0.0131301.
Values are sent between devices in bfloat16 or wider.
A program may use at most 1.5 GiB of HBM per device.

v0:
```python
import jax
import jax.numpy as jnp
from jax import lax
from jax.sharding import PartitionSpec as P


def sample_gram(row_data, micro_size):
    sample_mats = row_data.reshape(micro_size, -1, row_data.shape[-1])
    return jnp.einsum('mtd,msd->mts', sample_mats, sample_mats, preferred_element_type=jnp.float32)


def microbatch_sums(x_mb, dy_mb, len_mb, w_one, w_two, clip_norm):
    micro_size, seq_len, model_width = x_mb.shape
    layers = w_one.shape[0]
    row_count = micro_size * seq_len
    keep_mask = lax.broadcasted_iota(jnp.int32, (micro_size, seq_len), 1) < len_mb[:, None]
    dy_cur = jnp.where(keep_mask[:, :, None], dy_mb, jnp.zeros_like(dy_mb)).reshape(row_count, model_width)
    x_cur = x_mb.reshape(row_count, model_width)
    x_saved = []
    pre_saved = []
    act_saved = []
    for layer_idx in range(layers):
        pre_act = jnp.dot(x_cur, w_one[layer_idx], preferred_element_type=jnp.float32).astype(jnp.bfloat16)
        act_out = jax.nn.gelu(pre_act.astype(jnp.float32)).astype(jnp.bfloat16)
        x_saved.append(x_cur)
        pre_saved.append(pre_act)
        act_saved.append(act_out)
        if layer_idx < layers - 1:
            branch = jnp.dot(act_out, w_two[layer_idx], preferred_element_type=jnp.float32)
            x_cur = (x_cur.astype(jnp.float32) + branch).astype(jnp.bfloat16)
    dpre_saved = [None] * layers
    dy_saved = [None] * layers
    total_norm = jnp.zeros((micro_size,), jnp.float32)
    for layer_idx in reversed(range(layers)):
        d_act = jnp.einsum('nd,fd->nf', dy_cur, w_two[layer_idx], preferred_element_type=jnp.float32)
        _, gelu_back = jax.vjp(jax.nn.gelu, pre_saved[layer_idx].astype(jnp.float32))
        d_pre = gelu_back(d_act)[0].astype(jnp.bfloat16)
        norm_one = jnp.sum(sample_gram(x_saved[layer_idx], micro_size) * sample_gram(d_pre, micro_size), axis=(1, 2))
        norm_two = jnp.sum(sample_gram(act_saved[layer_idx], micro_size) * sample_gram(dy_cur, micro_size), axis=(1, 2))
        total_norm = total_norm + norm_one + norm_two
        dpre_saved[layer_idx] = d_pre
        dy_saved[layer_idx] = dy_cur
        if layer_idx > 0:
            d_back = jnp.einsum('nf,df->nd', d_pre, w_one[layer_idx], preferred_element_type=jnp.float32)
            dy_cur = (dy_cur.astype(jnp.float32) + d_back).astype(jnp.bfloat16)
    factor = jnp.minimum(1.0, clip_norm[0] / jnp.sqrt(total_norm))
    row_factor = jnp.broadcast_to(factor[:, None], (micro_size, seq_len)).reshape(row_count, 1)
    sum_pairs = []
    for layer_idx in range(layers):
        scaled_pre = (dpre_saved[layer_idx].astype(jnp.float32) * row_factor).astype(jnp.bfloat16)
        scaled_dy = (dy_saved[layer_idx].astype(jnp.float32) * row_factor).astype(jnp.bfloat16)
        grad_in = jnp.einsum('nd,nf->df', x_saved[layer_idx], scaled_pre, preferred_element_type=jnp.float32)
        grad_out = jnp.einsum('nf,nd->fd', act_saved[layer_idx], scaled_dy, preferred_element_type=jnp.float32)
        sum_pairs.append((grad_in, grad_out))
    return sum_pairs


def solution(mesh):
    data_size = mesh.shape['data']

    def device_body(x_loc, dy_loc, len_loc, w_one, w_two, noise_one, noise_two, clip_norm):
        samples = x_loc.shape[0]
        micro_size = samples // 2
        batch_total = samples * data_size
        first_sums = microbatch_sums(x_loc[:micro_size], dy_loc[:micro_size], len_loc[:micro_size], w_one, w_two, clip_norm)
        second_sums = microbatch_sums(x_loc[micro_size:], dy_loc[micro_size:], len_loc[micro_size:], w_one, w_two, clip_norm)
        out_one = []
        out_two = []
        for layer_idx in range(w_one.shape[0]):
            part_one = (first_sums[layer_idx][0] + second_sums[layer_idx][0]).astype(jnp.bfloat16)
            part_two = (first_sums[layer_idx][1] + second_sums[layer_idx][1]).astype(jnp.bfloat16)
            total_one = lax.psum(part_one, 'data')
            total_two = lax.psum(part_two, 'data')
            out_one.append((total_one.astype(jnp.float32) + noise_one[layer_idx]) / batch_total)
            out_two.append((total_two.astype(jnp.float32) + noise_two[layer_idx]) / batch_total)
        return jnp.stack(out_one), jnp.stack(out_two)

    return jax.shard_map(device_body, mesh=mesh, in_specs=(P('data'), P('data'), P('data'), P(), P(), P(), P(), P()), out_specs=(P(), P()), check_vma=False)
```

profile of v0, /device:TPU:0, one launch (start us, length us, event | category | flops | bytes accessed | tf_op | source)
XLA Modules:
  0.0 2033.0 jit_solution(5300958664866588324)
XLA Ops:
  113.1 23.4 %fusion.22 = bf16[1024,4096]{1,0:T(8,128)(2,1)} fusion(bf16[1024,4096]{1,0:T(8,128)(2,1)} %fusion.187, bf16[4,4096,1024]{2,1,0:T(8,128)(2,1)} %param.12, bf16[2,1024,1024]{2,1,0:T(8,128)(2,1)S(1)} %copy-done.2, pred[1024]{0:T(1024)(128)(4,1)S(1)} %iota_compare_fusion.1), kind=kOutput, calls=%fused_computation.64 | convolution fusion | flops 8679063552 | bytes 27264000 | tf_op jit(solution)/shard_map/nd,fd->nf/dot_general | solution.py:35
  150.4 24.2 %fusion.25 = bf16[1024,4096]{1,0:T(8,128)(2,1)} fusion(bf16[1024,4096]{1,0:T(8,128)(2,1)} %copy-done.56, bf16[1024,1024]{1,0:T(8,128)(2,1)S(1)} %fusion.237, bf16[4,4096,1024]{2,1,0:T(8,128)(2,1)} %param.12), kind=kOutput, calls=%fused_computation.67 | convolution fusion | flops 8678014976 | bytes 27262976 | tf_op jit(solution)/shard_map/nd,fd->nf/dot_general | solution.py:35
  188.6 24.3 %fusion.28 = bf16[1024,4096]{1,0:T(8,128)(2,1)} fusion(bf16[1024,4096]{1,0:T(8,128)(2,1)} %copy-done.57, bf16[1024,1024]{1,0:T(8,128)(2,1)S(1)} %fusion.239, bf16[4,4096,1024]{2,1,0:T(8,128)(2,1)} %param.12), kind=kOutput, calls=%fused_computation.70 | convolution fusion | flops 8678014976 | bytes 27262976 | tf_op jit(solution)/shard_map/nd,fd->nf/dot_general | solution.py:35
  232.6 24.5 %fusion.31 = bf16[1024,4096]{1,0:T(8,128)(2,1)} fusion(bf16[1024,4096]{1,0:T(8,128)(2,1)} %copy-done.58, bf16[1024,1024]{1,0:T(8,128)(2,1)} %copy-done.51, bf16[4,4096,1024]{2,1,0:T(8,128)(2,1)} %param.12), kind=kOutput, calls=%fused_computation.73 | convolution fusion | flops 8678014976 | bytes 27262976 | tf_op jit(solution)/shard_map/nd,fd->nf/dot_general | solution.py:35
  302.6 16.3 add_convert_fusion.10
  393.7 23.5 %fusion.10 = bf16[1024,4096]{1,0:T(8,128)(2,1)} fusion(bf16[1024,4096]{1,0:T(8,128)(2,1)} %fusion.190, bf16[4,4096,1024]{2,1,0:T(8,128)(2,1)} %param.12, bf16[2,1024,1024]{2,1,0:T(8,128)(2,1)S(1)} %copy-done.4, pred[1024]{0:T(1024)(128)(4,1)S(1)} %iota_compare_fusion), kind=kOutput, calls=%fused_computation.52 | convolution fusion | flops 8679063552 | bytes 27264000 | tf_op jit(solution)/shard_map/nd,fd->nf/dot_general | solution.py:35
  431.1 24.2 %fusion.13 = bf16[1024,4096]{1,0:T(8,128)(2,1)} fusion(bf16[1024,4096]{1,0:T(8,128)(2,1)} %copy-done.54, bf16[1024,1024]{1,0:T(8,128)(2,1)S(1)} %fusion.243, bf16[4,4096,1024]{2,1,0:T(8,128)(2,1)} %param.12), kind=kOutput, calls=%fused_computation.55 | convolution fusion | flops 8678014976 | bytes 27262976 | tf_op jit(solution)/shard_map/nd,fd->nf/dot_general | solution.py:35
  469.3 24.3 %fusion.16 = bf16[1024,4096]{1,0:T(8,128)(2,1)} fusion(bf16[1024,4096]{1,0:T(8,128)(2,1)} %copy-done.55, bf16[1024,1024]{1,0:T(8,128)(2,1)S(1)} %fusion.245, bf16[4,4096,1024]{2,1,0:T(8,128)(2,1)} %param.12), kind=kOutput, calls=%fused_computation.58 | convolution fusion | flops 8678014976 | bytes 27262976 | tf_op jit(solution)/shard_map/nd,fd->nf/dot_general | solution.py:35
  513.3 24.5 %fusion.19 = bf16[1024,4096]{1,0:T(8,128)(2,1)} fusion(bf16[1024,4096]{1,0:T(8,128)(2,1)} %fusion.172, bf16[1024,1024]{1,0:T(8,128)(2,1)} %copy-done.36, bf16[4,4096,1024]{2,1,0:T(8,128)(2,1)} %param.12), kind=kOutput, calls=%fused_computation.61 | convolution fusion | flops 8678014976 | bytes 27262976 | tf_op jit(solution)/shard_map/nd,fd->nf/dot_general | solution.py:35
  569.0 21.9 %multiply_reduce_fusion.8 = f32[]{:T(128)} fusion(f32[1024,1024]{1,0:T(8,128)S(1)} %copy-done.23, bf16[1024,4096]{1,0:T(8,128)(2,1)} %copy-done.58), kind=kOutput, calls=%fused_computation.308 | convolution fusion | flops 8633974784 | bytes 12582916 | tf_op jit(solution)/shard_map/mtd,msd->mts/dot_general | solution.py:9
  590.9 17.2 multiply_reduce_fusion.11
  608.0 16.5 multiply_reduce_fusion.15
  624.5 23.1 %multiply_reduce_fusion.14 = f32[]{:T(128)} fusion(f32[1024,1024]{1,0:T(8,128)} %fusion.296, bf16[1024,4096]{1,0:T(8,128)(2,1)} %fusion.187), kind=kOutput, calls=%fused_computation.314 | convolution fusion | flops 8633974784 | bytes 12582916 | tf_op jit(solution)/shard_map/mtd,msd->mts/dot_general | solution.py:9
  647.6 15.7 multiply_reduce_fusion.13
  663.4 23.4 %multiply_reduce_fusion.12 = f32[]{:T(128)} fusion(f32[1024,1024]{1,0:T(8,128)} %fusion.339, bf16[1024,4096]{1,0:T(8,128)(2,1)} %copy-done.56), kind=kOutput, calls=%fused_computation.312 | convolution fusion | flops 8633974784 | bytes 12582916 | tf_op jit(solution)/shard_map/mtd,msd->mts/dot_general | solution.py:9
  686.8 21.9 %multiply_reduce_fusion.10 = f32[]{:T(128)} fusion(f32[1024,1024]{1,0:T(8,128)S(1)} %copy-done.21, bf16[1024,4096]{1,0:T(8,128)(2,1)} %copy-done.57), kind=kOutput, calls=%fused_computation.310 | convolution fusion | flops 8633974784 | bytes 12582916 | tf_op jit(solution)/shard_map/mtd,msd->mts/dot_general | solution.py:9
  708.7 17.1 multiply_reduce_fusion.9
  731.6 19.0 fusion.273
  750.6 18.8 fusion.277
  785.0 19.2 fusion.281
  860.8 21.9 %multiply_reduce_fusion = f32[]{:T(128)} fusion(f32[1024,1024]{1,0:T(8,128)S(1)} %copy-done.20, bf16[1024,4096]{1,0:T(8,128)(2,1)} %fusion.172), kind=kOutput, calls=%fused_computation.297 | convolution fusion | flops 8633974784 | bytes 12582916 | tf_op jit(solution)/shard_map/mtd,msd->mts/dot_general | solution.py:9
  882.7 17.1 multiply_reduce_fusion.7
  899.8 22.2 %multiply_reduce_fusion.6 = f32[]{:T(128)} fusion(f32[1024,1024]{1,0:T(8,128)S(1)} %copy-done.53, bf16[1024,4096]{1,0:T(8,128)(2,1)} %fusion.190), kind=kOutput, calls=%fused_computation.303 | convolution fusion | flops 8633974784 | bytes 12582916 | tf_op jit(solution)/shard_map/mtd,msd->mts/dot_general | solution.py:9
  922.0 17.2 multiply_reduce_fusion.5
  939.1 22.1 %multiply_reduce_fusion.4 = f32[]{:T(128)} fusion(f32[1024,1024]{1,0:T(8,128)S(1)} %copy-done.19, bf16[1024,4096]{1,0:T(8,128)(2,1)} %copy-done.54), kind=kOutput, calls=%fused_computation.301 | convolution fusion | flops 8633974784 | bytes 12582916 | tf_op jit(solution)/shard_map/mtd,msd->mts/dot_general | solution.py:9
  961.2 17.0 multiply_reduce_fusion.3
  978.3 21.8 %multiply_reduce_fusion.2 = f32[]{:T(128)} fusion(f32[1024,1024]{1,0:T(8,128)S(1)} %copy-done.18, bf16[1024,4096]{1,0:T(8,128)(2,1)} %copy-done.55), kind=kOutput, calls=%fused_computation.299 | convolution fusion | flops 8633974784 | bytes 12582916 | tf_op jit(solution)/shard_map/mtd,msd->mts/dot_general | solution.py:9
  1000.1 17.1 multiply_reduce_fusion.1
  1022.3 20.6 %add_convert_fusion.3 = bf16[4096,1024]{1,0:T(8,128)(2,1)} fusion(f32[4096,1024]{1,0:T(8,128)} %fusion.273, bf16[1024,1024]{1,0:T(8,128)(2,1)S(1)} %copy-done.37, f32[]{:T(128)} %bitcast.17, bf16[1024,4096]{1,0:T(8,128)(2,1)} %fusion.172), kind=kOutput, calls=%fused_computation.149 | convolution fusion | flops 8643411968 | bytes 35651588 | tf_op jit(solution)/shard_map/nf,nd->fd/dot_general | solution.py:53
  1042.9 20.6 %add_convert_fusion.2 = bf16[4096,1024]{1,0:T(8,128)(2,1)} fusion(f32[4096,1024]{1,0:T(8,128)} %fusion.277, bf16[1024,1024]{1,0:T(8,128)(2,1)S(1)} %copy-done.35, f32[]{:T(128)} %bitcast.17, bf16[1024,4096]{1,0:T(8,128)(2,1)} %copy-done.55), kind=kOutput, calls=%fused_computation.148 | convolution fusion | flops 8643411968 | bytes 35651588 | tf_op jit(solution)/shard_map/nf,nd->fd/dot_general | solution.py:53
  1063.5 21.3 %add_convert_fusion.1 = bf16[4096,1024]{1,0:T(8,128)(2,1)} fusion(f32[4096,1024]{1,0:T(8,128)} %fusion.279, bf16[1024,1024]{1,0:T(8,128)(2,1)} %copy-done.33, f32[]{:T(128)} %bitcast.17, bf16[1024,4096]{1,0:T(8,128)(2,1)} %copy-done.54), kind=kOutput, calls=%fused_computation.147 | convolution fusion | flops 8643411968 | bytes 35651588 | tf_op jit(solution)/shard_map/nf,nd->fd/dot_general | solution.py:53
  1084.8 21.4 %add_convert_fusion = bf16[4096,1024]{1,0:T(8,128)(2,1)} fusion(f32[4096,1024]{1,0:T(8,128)} %fusion.281, f32[]{:T(128)} %bitcast.17, bf16[1024,4096]{1,0:T(8,128)(2,1)} %fusion.190, bf16[2,1024,1024]{2,1,0:T(8,128)(2,1)S(1)} %copy-done.7, pred[1024]{0:T(1024)(128)(4,1)S(1)} %copy-done.14), kind=kOutput, calls=%fused_computation.146 | convolution fusion | flops 8644460544 | bytes 35652612 | tf_op jit(solution)/shard_map/nf,nd->fd/dot_general | solution.py:53
  1106.2 17.5 fusion.98
  1123.8 17.6 add_convert_fusion.6
  1141.4 17.7 add_convert_fusion.5
  1159.1 17.6 add_convert_fusion.4
  1176.7 45.6 %fusion.335 = (f32[1,1024,4096]{2,1,0:T(8,128)}, f32[1,1024,4096]{2,1,0:T(8,128)}, f32[1,1024,4096]{2,1,0:T(8,128)}, f32[1,1024,4096]{2,1,0:T(8,128)}) fusion(f32[4,1024,4096]{2,1,0:T(8,128)} %param.13), kind=kLoop, calls=%fused_computation.357 | loop fusion | bytes 134217728 | tf_op jit(solution)/shard_map/slice | solution.py:74
  1222.3 17.5 copy.27
  1239.8 17.5 copy.28
  1257.2 17.4 copy.29
  1274.7 17.4 copy.30
  1292.1 474.4 %all-reduce.3.cloned.1.call-done = (bf16[1024,4096]{0,1:T(8,128)(2,1)}, bf16[1024,4096]{0,1:T(8,128)(2,1)}, bf16[1024,4096]{0,1:T(8,128)(2,1)}, bf16[1024,4096]{...) async-done(((bf16[1024,4096]{0,1:T(8,128)(2,1)}, ...) | async-done | bytes 67108880 | tf_op jit(solution)/shard_map/psum | solution.py:72
  1766.5 28.4 %fusion.93 = (f32[1,1024,4096]{1,2,0:T(8,128)}, f32[1,1024,4096]{1,2,0:T(8,128)}) fusion(f32[1,1024,4096]{1,2,0:T(8,128)} %copy.28, bf16[1024,4096]{0,1:T(8,128)(2,1)} %get-tuple-element.6, f32[1,1024,4096]{1,2,0:T(8,128)} %copy.27, bf16[1024,4096]{0,1:T(8,128)(2,1)} %get-tuple-element.7), kind=kLoop, calls=%fused_computation.142 | loop fusion | flops 25165824 | bytes 83886080 | tf_op jit(solution)/shard_map/stack | solution.py:76
  1795.9 24.7 %fusion.89 = (f32[1,1024,4096]{1,2,0:T(8,128)}, f32[1,1024,4096]{1,2,0:T(8,128)}) fusion(f32[1,1024,4096]{1,2,0:T(8,128)} %copy.30, bf16[1024,4096]{0,1:T(8,128)(2,1)S(1)} %copy-done, f32[1,1024,4096]{1,2,0:T(8,128)} %copy.29, bf16[1024,4096]{0,1:T(8,128)(2,1)} %get-tuple-element.5), kind=kLoop, calls=%fused_computation.136 | loop fusion | flops 25165824 | bytes 83886080 | tf_op jit(solution)/shard_map/stack | solution.py:76
  1820.6 44.3 %pad_maximum_fusion = f32[4,1024,4096]{1,2,0:T(8,128)} fusion(f32[1,1024,4096]{1,2,0:T(8,128)} %get-tuple-element.22, f32[1,1024,4096]{1,2,0:T(8,128)} %get-tuple-element.23, f32[1,1024,4096]{1,2,0:T(8,128)} %get-tuple-element.24, f32[1,1024,4096]{1,2,0:T(8,128)} %get-tuple-element.25), kind=kLoop, calls=%fused_computation | loop fusion | flops 50331648 | bytes 134217728 | tf_op jit(solution)/shard_map/stack | solution.py:76
  1864.9 61.2 %copy.20 = f32[4,1024,4096]{2,1,0:T(8,128)} copy(f32[4,1024,4096]{1,2,0:T(8,128)} %pad_maximum_fusion) | data formatting | bytes 134217728
  1926.0 55.4 %fusion.87 = (f32[1,4096,1024]{2,1,0:T(8,128)}, f32[1,4096,1024]{2,1,0:T(8,128)}, f32[1,4096,1024]{2,1,0:T(8,128)}, f32[1,4096,1024]{2,1,0:T(8,128)}) fusion(f32[4,4096,1024]{2,1,0:T(8,128)} %param.14, bf16[4096,1024]{1,0:T(8,128)(2,1)} %get-tuple-element.11, bf16[4096,1024]{1,0:T(8,128)(2,1)} %get-tuple-element.10, ...), kind=kLoop, calls=%fused_computation.133 | loop fusion | flops 50331648 | bytes 167772160 | tf_op jit(solution)/shard_map/stack | solution.py:76
  1981.4 44.4 %pad_maximum_fusion.1 = f32[4,4096,1024]{2,1,0:T(8,128)} fusion(f32[1,4096,1024]{2,1,0:T(8,128)} %get-tuple-element.14, f32[1,4096,1024]{2,1,0:T(8,128)} %get-tuple-element.15, f32[1,4096,1024]{2,1,0:T(8,128)} %get-tuple-element.13, f32[1,4096,1024]{2,1,0:T(8,128)} %get-tuple-element.12), kind=kLoop, calls=%fused_computation.1 | loop fusion | flops 50331648 | bytes 134217728 | tf_op jit(solution)/shard_map/stack | solution.py:76
  (173 shorter events, 425.2 us)
Async XLA Ops:
  7.2 1759.4 %all-reduce.3.cloned.1.call-start = ((), (), s32[]{:S(2)}) async-start(), calls=%async_computation | async-start | bytes 134217728 | tf_op jit(solution)/shard_map/psum | solution.py:72
  7.2 16.1 copy-start.8
  37.4 12.0 copy-start.44
  66.6 12.0 copy-start.41
  96.1 15.7 copy-start.38
  96.1 15.7 copy-start.1
  96.1 17.0 copy-start.2
  113.0 23.4 %copy-start.15 = (pred[1024]{0:T(1024)(128)(4,1)}, pred[1024]{0:T(1024)(128)(4,1)S(1)}, u32[]{:S(2)}) copy-start(pred[1024]{0:T(1024)(128)(4,1)S(1)} %iota_compare_fusion.1) | copy-start | bytes 3076
  150.4 128.7 %copy-start.47 = (bf16[1024,1024]{1,0:T(8,128)(2,1)}, bf16[1024,1024]{1,0:T(8,128)(2,1)S(1)}, u32[]{:S(2)}) copy-start(bf16[1024,1024]{1,0:T(8,128)(2,1)S(1)} %fusion.237) | copy-start | bytes 6291460
  188.6 94.9 %copy-start.49 = (bf16[1024,1024]{1,0:T(8,128)(2,1)}, bf16[1024,1024]{1,0:T(8,128)(2,1)S(1)}, u32[]{:S(2)}) copy-start(bf16[1024,1024]{1,0:T(8,128)(2,1)S(1)} %fusion.239) | copy-start | bytes 6291460
  232.6 24.5 %copy-start.9 = (bf16[2,1024,1024]{2,1,0:T(8,128)(2,1)S(1)}, bf16[2,1024,1024]{2,1,0:T(8,128)(2,1)}, u32[]{:S(2)}) copy-start(bf16[2,1024,1024]{2,1,0:T(8,128)(2,1)} %param.8) | copy-start | bytes 12582916
  318.9 12.0 copy-start.30
  348.2 12.0 copy-start.28
  377.4 15.7 copy-start.25
  377.4 16.3 copy-start.4
  393.7 23.5 %copy-start.12 = (pred[1024]{0:T(1024)(128)(4,1)}, pred[1024]{0:T(1024)(128)(4,1)S(1)}, u32[]{:S(2)}) copy-start(pred[1024]{0:T(1024)(128)(4,1)S(1)} %iota_compare_fusion) | copy-start | bytes 3076
  431.1 124.4 %copy-start.33 = (bf16[1024,1024]{1,0:T(8,128)(2,1)}, bf16[1024,1024]{1,0:T(8,128)(2,1)S(1)}, u32[]{:S(2)}) copy-start(bf16[1024,1024]{1,0:T(8,128)(2,1)S(1)} %fusion.243) | copy-start | bytes 6291460
  469.3 94.9 %copy-start.34 = (bf16[1024,1024]{1,0:T(8,128)(2,1)}, bf16[1024,1024]{1,0:T(8,128)(2,1)S(1)}, u32[]{:S(2)}) copy-start(bf16[1024,1024]{1,0:T(8,128)(2,1)S(1)} %fusion.245) | copy-start | bytes 6291460
  513.3 24.5 %copy-start.10 = (bf16[2,1024,1024]{2,1,0:T(8,128)(2,1)S(1)}, bf16[2,1024,1024]{2,1,0:T(8,128)(2,1)}, u32[]{:S(2)}) copy-start(bf16[2,1024,1024]{2,1,0:T(8,128)(2,1)} %param.8) | copy-start | bytes 12582916
  542.3 8.8 copy-start.29
  559.8 9.2 copy-start.23
  590.8 17.2 copy-start.24
  624.5 23.1 %copy-start.22 = (f32[1024,1024]{1,0:T(8,128)S(1)}, f32[1024,1024]{1,0:T(8,128)}, u32[]{:S(2)}) copy-start(f32[1024,1024]{1,0:T(8,128)} %fusion.338) | copy-start | bytes 12582916
  663.4 23.4 %copy-start.21 = (f32[1024,1024]{1,0:T(8,128)S(1)}, f32[1024,1024]{1,0:T(8,128)}, u32[]{:S(2)}) copy-start(f32[1024,1024]{1,0:T(8,128)} %fusion.341) | copy-start | bytes 12582916
  708.7 22.8 %copy-start.52 = (bf16[1024,1024]{1,0:T(8,128)(2,1)S(1)}, bf16[1024,1024]{1,0:T(8,128)(2,1)}, u32[]{:S(2)}) copy-start(bf16[1024,1024]{1,0:T(8,128)(2,1)} %copy-done.51) | copy-start | bytes 6291460
  731.6 19.1 copy-start.50
  731.6 37.9 %slice-start.2 = ((s8[8388608]{0:T(1024)(128)(4,1)}), s8[4194304]{0:T(1024)(128)(4,1)S(1)}, s32[]{:S(2)}) async-start(s8[8388608]{0:T(1024)(128)(4,1)} %bitcast.294), calls=%async_computation.3 | async-start | bytes 8388608
  750.6 18.8 copy-start.48
  750.6 18.8 slice-start.3
  769.5 15.5 copy-start.6
  769.5 15.5 copy-start.17
  785.0 19.2 copy-start.11
  785.0 48.9 %slice-start = ((s8[8388608]{0:T(1024)(128)(4,1)}), s8[4194304]{0:T(1024)(128)(4,1)S(1)}, s32[]{:S(2)}) async-start(s8[8388608]{0:T(1024)(128)(4,1)} %bitcast.292), calls=%async_computation.1 | async-start | bytes 8388608
  804.2 14.9 copy-start.46
  804.2 29.7 %slice-start.1 = ((s8[8388608]{0:T(1024)(128)(4,1)}), s8[4194304]{0:T(1024)(128)(4,1)S(1)}, s32[]{:S(2)}) async-start(s8[8388608]{0:T(1024)(128)(4,1)} %bitcast.292), calls=%async_computation.2 | async-start | bytes 8388608
  819.1 14.7 copy-start.43
  833.9 11.7 copy-start.40
  845.5 15.3 copy-start.20
  882.7 17.1 copy-start.53
  922.0 17.2 copy-start.19
  961.2 17.0 copy-start.18
  1000.1 22.2 %copy-start.37 = (bf16[1024,1024]{1,0:T(8,128)(2,1)S(1)}, bf16[1024,1024]{1,0:T(8,128)(2,1)}, u32[]{:S(2)}) copy-start(bf16[1024,1024]{1,0:T(8,128)(2,1)} %copy-done.36) | copy-start | bytes 6291460
  1022.3 20.6 %copy-start.35 = (bf16[1024,1024]{1,0:T(8,128)(2,1)S(1)}, bf16[1024,1024]{1,0:T(8,128)(2,1)}, u32[]{:S(2)}) copy-start(bf16[1024,1024]{1,0:T(8,128)(2,1)} %copy-done.34) | copy-start | bytes 6291460
  1063.5 21.3 %copy-start.7 = (bf16[2,1024,1024]{2,1,0:T(8,128)(2,1)S(1)}, bf16[2,1024,1024]{2,1,0:T(8,128)(2,1)}, u32[]{:S(2)}) copy-start(bf16[2,1024,1024]{2,1,0:T(8,128)(2,1)} %param.9) | copy-start | bytes 12582916
  1063.5 21.3 %copy-start.14 = (pred[1024]{0:T(1024)(128)(4,1)S(1)}, pred[1024]{0:T(1024)(128)(4,1)}, u32[]{:S(2)}) copy-start(pred[1024]{0:T(1024)(128)(4,1)} %copy-done.12) | copy-start | bytes 3076
  1106.2 17.5 copy-start.32
  1141.4 17.7 copy-start.27
  1766.5 29.4 %copy-start = (bf16[1024,4096]{0,1:T(8,128)(2,1)S(1)}, bf16[1024,4096]{0,1:T(8,128)(2,1)}, u32[]{:S(2)}) copy-start(bf16[1024,4096]{0,1:T(8,128)(2,1)} %get-tuple-element.4) | copy-start | bytes 25165828
  (16 other events, 88.7 us)
Sparse Core Ops, SparseCore 0:
  1176.8 589.6 all-reduce.2
where the time goes:
time: 2040 us; the launch traced here: 2030 us
  matrix products  1140 us (56%)
  waiting for transfers between devices  474 us (23%)
  other arithmetic  198 us (10%)
  local copies, waits for them, and re-layouts  197 us (10%)
  between operations  25.7 us (1%)
    psum x1, waiting for transfers between devices, device_body(): total_one = lax.psum(part_one, 'data')  474 us
    dot_general x32, matrix products, sample_gram(): jnp.einsum('mtd,msd->mts', sample_mats, sample_mats, preferred_element_ty...  384 us
    another operation x5, other arithmetic, device_body(): return (jnp.stack(out_one), jnp.stack(out_two))  197 us
    dot_general x8, matrix products, microbatch_sums(): jnp.einsum('nd,fd->nf', dy_cur, w_two[layer_idx], preferred_element_type=...  193 us
    dot_general x8, matrix products, microbatch_sums(): jnp.einsum('nf,nd->fd', act_saved[layer_idx], scaled_dy, preferred_elemen...  156 us
    unnamed x131, local copies, waits for them, and re-layouts  151 us
    dot_general x8, matrix products, microbatch_sums(): jnp.einsum('nd,nf->df', x_saved[layer_idx], scaled_pre, preferred_element...  127 us
    dot_general x8, matrix products, microbatch_sums(): jnp.dot(x_cur, w_one[layer_idx], preferred_element_type=jnp.float32)  106 us
  transfers between devices with their start and end apart: 1, of which 1 were waited for; matrix products, arithmetic and copies ran while one was open for 6% of the time, Pallas kernels for 0%

commit v1 on v0

v1 whole, which is shorter than its diff:
```python
import functools

import jax
import jax.numpy as jnp
from jax import lax
from jax.experimental import pallas as pl
from jax.experimental.pallas import tpu as pltpu
from jax.sharding import PartitionSpec as P

BF16 = jnp.bfloat16
F32 = jnp.float32
VMEM_LIMIT = 66_000_000
C0 = 0.7978845608028654
C1 = 0.044715
NT = (((1,), (1,)), ((), ()))


def gelu_tanh(x):
    half = 0.5 * x
    return half + half * jnp.tanh(x * (C0 + (C0 * C1) * (x * x)))


def gelu_tanh_grad(x):
    sq = x * x
    t = jnp.tanh(x * (C0 + (C0 * C1) * sq))
    return (1.0 + t) * (0.5 + (x * (0.5 * C0 + (1.5 * C0 * C1) * sq)) * (1.0 - t))


def params(dims):
    return pltpu.CompilerParams(vmem_limit_bytes=VMEM_LIMIT, dimension_semantics=("arbitrary",) * dims)


def forward_kernel(tm, sub, x_ref, w1_ref, w2_ref, xs_ref, h_ref, a_ref, xcur):
    layer, m = pl.program_id(0), pl.program_id(1)
    last = pl.num_programs(0) - 1
    rows = pl.ds(pl.multiple_of(m * tm, tm), tm)

    def up():
        xs_ref[0] = jnp.where(layer == 0, x_ref[...], xcur[rows, :])
        for s in range(w1_ref.shape[-1] // sub):
            cols = slice(s * sub, (s + 1) * sub)
            h = jnp.dot(xs_ref[0], w1_ref[0, :, cols], preferred_element_type=F32).astype(BF16)
            h_ref[0, :, cols] = h
            a_ref[0, :, cols] = gelu_tanh(h.astype(F32)).astype(BF16)

    @pl.when(layer < last)
    def _():
        up()
        for s in range(w2_ref.shape[-1] // sub):
            cols = slice(s * sub, (s + 1) * sub)
            branch = jnp.dot(a_ref[0], w2_ref[0, :, cols], preferred_element_type=F32)
            xcur[rows, cols] = (xs_ref[0, :, cols].astype(F32) + branch).astype(BF16)

    @pl.when(layer == last)
    def _():
        up()


def forward_stack(x, w1, w2, tm=512, sub=512):
    layers, dm, df = w1.shape
    m_rows = x.shape[0]
    nm = m_rows // tm
    return pl.pallas_call(
        functools.partial(forward_kernel, tm, sub),
        grid=(layers, nm),
        in_specs=[
            pl.BlockSpec((tm, dm), lambda l, m: (jnp.where(l == 0, m, nm - 1), 0)),
            pl.BlockSpec((1, dm, df), lambda l, m: (l, 0, 0)),
            pl.BlockSpec((1, df, dm), lambda l, m: (jnp.minimum(l, layers - 2), 0, 0)),
        ],
        out_specs=[
            pl.BlockSpec((1, tm, dm), lambda l, m: (l, m, 0)),
            pl.BlockSpec((1, tm, df), lambda l, m: (l, m, 0)),
            pl.BlockSpec((1, tm, df), lambda l, m: (l, m, 0)),
        ],
        out_shape=[
            jax.ShapeDtypeStruct((layers, m_rows, dm), BF16),
            jax.ShapeDtypeStruct((layers, m_rows, df), BF16),
            jax.ShapeDtypeStruct((layers, m_rows, df), BF16),
        ],
        scratch_shapes=[pltpu.VMEM((m_rows, dm), BF16)],
        compiler_params=params(2),
        name="forward_stack",
    )(x, w1, w2)


def backward_kernel(tm, sub, per, len_ref, d_ref, h_ref, w1_ref, w2_ref, ds_ref, e_ref, dcur):
    step, m = pl.program_id(0), pl.program_id(1)
    last = pl.num_programs(0) - 1
    rows = pl.ds(pl.multiple_of(m * tm, tm), tm)

    def to_hidden():
        limit = len_ref[m // per] - (m % per) * tm
        keep = lax.broadcasted_iota(jnp.int32, (tm, d_ref.shape[-1]), 0) < limit
        fresh = jnp.where(keep, d_ref[...].astype(F32), 0.0).astype(BF16)
        ds_ref[0] = jnp.where(step == 0, fresh, dcur[rows, :])
        for s in range(w1_ref.shape[-1] // sub):
            cols = slice(s * sub, (s + 1) * sub)
            da = lax.dot_general(ds_ref[0], w2_ref[0, cols, :], NT, preferred_element_type=F32)
            e_ref[0, :, cols] = (da * gelu_tanh_grad(h_ref[0, :, cols].astype(F32))).astype(BF16)

    @pl.when(step < last)
    def _():
        to_hidden()
        for s in range(w2_ref.shape[-1] // sub):
            cols = slice(s * sub, (s + 1) * sub)
            back = lax.dot_general(e_ref[0], w1_ref[0, cols, :], NT, preferred_element_type=F32)
            dcur[rows, cols] = (ds_ref[0, :, cols].astype(F32) + back).astype(BF16)

    @pl.when(step == last)
    def _():
        to_hidden()


def backward_stack(lengths, d, h, w1, w2, seq, tm=512, sub=512):
    layers, dm, df = w1.shape
    m_rows = d.shape[0]
    nm = m_rows // tm
    return pl.pallas_call(
        functools.partial(backward_kernel, tm, sub, seq // tm),
        grid=(layers, nm),
        in_specs=[
            pl.BlockSpec(memory_space=pltpu.SMEM),
            pl.BlockSpec((tm, dm), lambda s, m: (jnp.where(s == 0, m, nm - 1), 0)),
            pl.BlockSpec((1, tm, df), lambda s, m: (layers - 1 - s, m, 0)),
            pl.BlockSpec((1, dm, df), lambda s, m: (jnp.maximum(layers - 1 - s, 1), 0, 0)),
            pl.BlockSpec((1, df, dm), lambda s, m: (layers - 1 - s, 0, 0)),
        ],
        out_specs=[
            pl.BlockSpec((1, tm, dm), lambda s, m: (layers - 1 - s, m, 0)),
            pl.BlockSpec((1, tm, df), lambda s, m: (layers - 1 - s, m, 0)),
        ],
        out_shape=[
            jax.ShapeDtypeStruct((layers, m_rows, dm), BF16),
            jax.ShapeDtypeStruct((layers, m_rows, df), BF16),
        ],
        scratch_shapes=[pltpu.VMEM((m_rows, dm), BF16)],
        compiler_params=params(2),
        name="backward_stack",
    )(lengths, d, h, w1, w2)


def fold(v):
    return jnp.sum(v.reshape(v.shape[0] // 8, 8, v.shape[1] // 128, 128), axis=(0, 2))


def gram_kernel(bs, x_ref, e_ref, a_ref, d_ref, o_ref):
    seq = x_ref.shape[0]
    once = jnp.zeros((8, 128), F32)
    twice = jnp.zeros((8, 128), F32)

    def block(ref, r0, r1, c0, c1):
        return lax.dot_general(ref[r0:r1, :], ref[c0:c1, :], NT, preferred_element_type=F32)

    for j in range(seq // bs):
        c0, c1 = j * bs, (j + 1) * bs
        for p, q in ((x_ref, e_ref), (d_ref, a_ref)):
            if j:
                twice += fold(block(p, 0, c0, c0, c1) * block(q, 0, c0, c0, c1))
            once += fold(block(p, c0, c1, c0, c1) * block(q, c0, c1, c0, c1))
    o_ref[0, 0] = once + 2.0 * twice


def gram_norms(x, e, a, d, seq, bs=256):
    layers, m_rows = x.shape[:2]
    return pl.pallas_call(
        functools.partial(gram_kernel, bs),
        grid=(layers, m_rows // seq),
        in_specs=[pl.BlockSpec((None, seq, v.shape[-1]), lambda l, i: (l, i, 0)) for v in (x, e, a, d)],
        out_specs=pl.BlockSpec((1, 1, 8, 128), lambda l, i: (l, i, 0, 0)),
        out_shape=jax.ShapeDtypeStruct((layers, m_rows // seq, 8, 128), F32),
        compiler_params=params(2),
        name="gram_norms",
    )(x, e, a, d)


TN = (((0,), (0,)), ((), ()))
MESH_ID = pl.DeviceIdType.MESH
SLOTS = 6
AG_SLOTS = 24
QUARTERS = 4
LAG = 3
STAGES = 8


def grad_sum_kernel(seq, n_chunks, factor_ref, xs_ref, a_ref, d_ref, e_ref, tot1_ref, tot2_ref,
                    lhs, raw, rhs, part, sum1, sum2, sum3, got0, got1, got2, got3, full,
                    load_sem, out_sem, send_sem, recv_sem):
    me = lax.axis_index("data")
    rows_all, width = rhs.shape
    tile = part.shape[1]
    core = me % 2
    sibling = me + 1 - 2 * core
    per_layer = 2 * QUARTERS

    def place(n):
        block = n // QUARTERS
        layer = block // per_layer
        return block, layer, block % per_layer

    def weight(color):
        return 2 + 2 * color + color * (color - 1)

    def route(color):
        w1, w2, w3 = weight(color), weight((color + 1) % 3), weight((color + 2) % 3)
        b1, b2, b3 = (me // w1) % 2, (me // w2) % 2, (me // w3) % 2
        n1, n2, n3 = me + w1 * (1 - 2 * b1), me + w2 * (1 - 2 * b2), me + w3 * (1 - 2 * b3)
        return (b1, b2, b3), (n1, n2, n3)

    barrier = pltpu.get_barrier_semaphore()
    _, near = route(0)
    for other in (sibling,) + near:
        pl.semaphore_signal(barrier, inc=1, device_id=(other,), device_id_type=MESH_ID)
    pl.semaphore_wait(barrier, 4)

    def aligned(v):
        return pl.multiple_of(v, 16)

    def loads(block, start):
        layer, which = block // per_layer, block % per_layer
        cols = pl.ds(pl.multiple_of((which % QUARTERS) * width, width), width)
        slot = block % 2

        def go(left, right):
            for copy in (pltpu.make_async_copy(left, lhs.at[slot], load_sem.at[0]),
                         pltpu.make_async_copy(right, raw, load_sem.at[1])):
                if start:
                    copy.start()
                else:
                    copy.wait()

        @pl.when(which < QUARTERS)
        def _():
            go(xs_ref.at[layer], e_ref.at[layer, :, cols])

        @pl.when(which >= QUARTERS)
        def _():
            go(a_ref.at[layer, :, cols], d_ref.at[layer])

    def remote(stage, n, src, dst, device):
        slot = n % SLOTS
        return pltpu.make_async_remote_copy(
            src_ref=src, dst_ref=dst, send_sem=send_sem.at[stage, slot], recv_sem=recv_sem.at[stage, slot],
            device_id=(device,), device_id_type=MESH_ID)

    def transfer(n, stage):
        slot, ag = n % SLOTS, n % AG_SLOTS
        (b1, b2, b3), (n1, n2, n3) = route(n % 3)
        half, quarter, eighth, piece = tile // 2, tile // 4, tile // 8, tile // 16

        def pick(ref, bit, size):
            return ref.at[slot, pl.ds(aligned((1 - bit) * size), size), :]

        def own(start, size):
            return full.at[ag, pl.ds(aligned(start), size), :]

        p1 = core * half
        p2 = p1 + b1 * quarter
        p3 = p2 + b2 * eighth
        p4 = p3 + b3 * piece
        if stage < 4:
            src, bit, size, got, device = ((part, core, half, got0, sibling), (sum1, b1, quarter, got1, n1),
                                           (sum2, b2, eighth, got2, n2), (sum3, b3, piece, got3, n3))[stage]
            return remote(stage, n, pick(src, bit, size), got.at[slot], device)
        start, size, device = ((p4, piece, n3), (p3, eighth, n2), (p2, quarter, n1), (p1, half, sibling))[stage - 4]
        return remote(stage, n, own(start, size), own(start, size), device)

    def add(n, stage):
        slot, ag = n % SLOTS, n % AG_SLOTS
        (b1, b2, b3), _ = route(n % 3)
        half, quarter, eighth, piece = tile // 2, tile // 4, tile // 8, tile // 16
        src, bit, size, got = ((part, core, half, got0), (sum1, b1, quarter, got1),
                               (sum2, b2, eighth, got2), (sum3, b3, piece, got3))[stage]
        value = (src[slot, pl.ds(aligned(bit * size), size), :].astype(F32) + got[slot].astype(F32)).astype(BF16)
        if stage < 3:
            (sum1, sum2, sum3)[stage][slot] = value
        else:
            full[ag, pl.ds(aligned(core * half + b1 * quarter + b2 * eighth + b3 * piece), piece), :] = value

    def out_copy(n, start):
        block, layer, which = place(n)
        ag, row = n % AG_SLOTS, (n % QUARTERS) * tile

        def go(dst):
            copy = pltpu.make_async_copy(full.at[ag], dst, out_sem.at[n % SLOTS])
            if start:
                copy.start()
            else:
                copy.wait()

        @pl.when(which < QUARTERS)
        def _():
            go(tot1_ref.at[layer, pl.ds(aligned(row), tile), pl.ds(pl.multiple_of((which % QUARTERS) * width, width), width)])

        @pl.when(which >= QUARTERS)
        def _():
            go(tot2_ref.at[layer, pl.ds(aligned((which % QUARTERS) * width + row), tile), :])

    def guarded(t, offset, fn):
        n = t - offset

        @pl.when((n >= 0) & (n < n_chunks))
        def _():
            fn(n)

    loads(0, True)
    first = 1
    done = first + STAGES * LAG

    def tick(t, carry):
        guarded(t, done + LAG, lambda n: out_copy(n, False))
        for stage in range(STAGES):
            def arrive(n, stage=stage):
                transfer(n, stage).wait()
                if stage < 4:
                    add(n, stage)
            guarded(t, first + LAG * (stage + 1), arrive)
        for stage in range(STAGES):
            guarded(t, first + LAG * stage, lambda n, stage=stage: transfer(n, stage).start())
        guarded(t, done, lambda n: out_copy(n, True))

        def compute(n):
            block = n // QUARTERS

            @pl.when(n % QUARTERS == 0)
            def _():
                loads(block, False)
                for i in range(rows_all // seq):
                    rhs[i * seq:(i + 1) * seq, :] = (raw[i * seq:(i + 1) * seq, :].astype(F32) * factor_ref[i]).astype(BF16)

                @pl.when(n + QUARTERS < n_chunks)
                def _():
                    loads(block + 1, True)

            cols = pl.ds(pl.multiple_of((n % QUARTERS) * tile, tile), tile)
            part[n % SLOTS] = lax.dot_general(lhs[block % 2, :, cols], rhs[...], TN, preferred_element_type=F32).astype(BF16)
        guarded(t, 0, compute)
        return carry

    lax.fori_loop(0, n_chunks + done + LAG, tick, 0)


def grad_sums(factor, xs, a, d, e, seq):
    layers, rows, dm = xs.shape
    df = a.shape[-1]
    tile = dm // QUARTERS
    n_chunks = layers * 2 * (df // dm) * QUARTERS
    hbm = pl.BlockSpec(memory_space=pl.ANY)

    def vmem(*shape):
        return pltpu.VMEM(shape, BF16)

    return pl.pallas_call(
        functools.partial(grad_sum_kernel, seq, n_chunks),
        in_specs=[pl.BlockSpec(memory_space=pltpu.SMEM), hbm, hbm, hbm, hbm],
        out_specs=[hbm, hbm],
        out_shape=[jax.ShapeDtypeStruct((layers, dm, df), BF16), jax.ShapeDtypeStruct((layers, df, dm), BF16)],
        scratch_shapes=[
            vmem(2, rows, dm), vmem(rows, dm), vmem(rows, dm),
            vmem(SLOTS, tile, dm), vmem(SLOTS, tile // 2, dm), vmem(SLOTS, tile // 4, dm), vmem(SLOTS, tile // 8, dm),
            vmem(SLOTS, tile // 2, dm), vmem(SLOTS, tile // 4, dm), vmem(SLOTS, tile // 8, dm), vmem(SLOTS, tile // 16, dm),
            vmem(AG_SLOTS, tile, dm),
            pltpu.SemaphoreType.DMA((2,)),
            pltpu.SemaphoreType.DMA((SLOTS,)),
            pltpu.SemaphoreType.DMA((STAGES, SLOTS)),
            pltpu.SemaphoreType.DMA((STAGES, SLOTS)),
        ],
        compiler_params=pltpu.CompilerParams(vmem_limit_bytes=VMEM_LIMIT, collective_id=0, has_side_effects=True),
        name="grad_sums",
    )(factor, xs, a, d, e)


def finish_kernel(scale, total_ref, noise_ref, out_ref):
    out_ref[...] = (total_ref[...].astype(F32) + noise_ref[...]) * scale


def finish(total, noise, scale):
    layers, rows, cols = noise.shape
    tile = (1 << 20) // cols
    return pl.pallas_call(
        functools.partial(finish_kernel, scale),
        grid=(layers, rows // tile),
        in_specs=[pl.BlockSpec((1, tile, cols), lambda l, r: (l, r, 0))] * 2,
        out_specs=pl.BlockSpec((1, tile, cols), lambda l, r: (l, r, 0)),
        out_shape=jax.ShapeDtypeStruct(noise.shape, F32),
        compiler_params=params(2),
        name="finish",
    )(total, noise)


def solution(mesh):
    devices = mesh.shape["data"]

    def body(x, dy, lengths, w1, w2, noise1, noise2, clip):
        samples, seq, dm = x.shape
        rows = samples * seq
        xs, h, a = forward_stack(x.reshape(rows, dm), w1, w2)
        d, e = backward_stack(lengths, dy.reshape(rows, dm), h, w1, w2, seq)
        norms = jnp.sum(gram_norms(xs, e, a, d, seq), axis=(0, 2, 3))
        factor = jnp.minimum(1.0, clip[0] / jnp.sqrt(norms))
        scale = 1.0 / (samples * devices)
        total1, total2 = grad_sums(factor, xs, a, d, e, seq)
        return finish(total1, noise1, scale), finish(total2, noise2, scale)

    data, whole = P("data"), P()
    return jax.shard_map(
        body,
        mesh=mesh,
        in_specs=(data, data, data, whole, whole, whole, whole, whole),
        out_specs=(whole, whole),
        check_vma=False,
    )
```

time: 2040 us -> 1040 us (0.51)
  matrix products: 1140 us -> 0 us
  Pallas kernels: 0 us -> 1030 us
  waiting for transfers between devices: 474 us -> 0 us
  local copies, waits for them, and re-layouts: 197 us -> 0 us
  other arithmetic: 198 us -> 1.38 us
  between operations: 25.7 us -> 1.74 us
    dot_general x76 -> x0, matrix products: 1140 us -> none  [the longest x32 384 us: sample_gram(): jnp.einsum('mtd,msd->mts', sample_mats, sample_mats, preferred_element_ty...]
    pallas_call x0 -> x6, Pallas kernels: none -> 1030 us  [the longest x1 450 us: grad_sums(): pl.pallas_call(functools.partial(grad_sum_kernel, seq, n_chunks), in_spec...]
    psum x1 -> x0, waiting for transfers between devices: 474 us -> none  [device_body(): total_one = lax.psum(part_one, 'data')]
    another operation x5 -> x0, other arithmetic: 197 us -> none  [device_body(): return (jnp.stack(out_one), jnp.stack(out_two))]
    unnamed x131 -> x0, local copies, waits for them, and re-layouts: 151 us -> none
    slice x2 -> x0, local copies, waits for them, and re-layouts: 46.2 us -> none  [the longest x1 45.6 us: device_body(): noise_one[layer_idx]]
  transfers between devices with their start and end apart: 1 -> 0, of which waited for: 1 -> 0; matrix products, arithmetic and copies ran while one was open for 6% -> 0% of each run, Pallas kernels for 0% -> 0%
where the time goes in v1:
time: 1040 us; the launch traced here: 1030 us
  Pallas kernels  1030 us (99%)
    pallas_call x1, Pallas kernels, grad_sums(): pl.pallas_call(functools.partial(grad_sum_kernel, seq, n_chunks), in_spec...  450 us
    pallas_call x1, Pallas kernels, backward_stack(): pl.pallas_call(functools.partial(backward_kernel, tm, sub, seq // tm), gr...  175 us
    pallas_call x1, Pallas kernels, forward_stack(): pl.pallas_call(functools.partial(forward_kernel, tm, sub), grid=(layers,...  164 us
    pallas_call x1, Pallas kernels, gram_norms(): pl.pallas_call(functools.partial(gram_kernel, bs), grid=(layers, m_rows /...  129 us
    pallas_call x2, Pallas kernels, finish(): pl.pallas_call(functools.partial(finish_kernel, scale), grid=(layers, row...  108 us

profile of v1, /device:TPU:0, one launch (start us, length us, event | category | flops | bytes accessed | tf_op | source)
XLA Modules:
  0.0 1028.9 jit_solution(9960704733339840264)
XLA Ops:
  1.3 163.6 %forward_stack.1 = (bf16[4,2048,1024]{2,1,0:T(8,128)(2,1)}, bf16[4,2048,4096]{2,1,0:T(8,128)(2,1)}, bf16[4,2048,4096]{2,1,0:T(8,128)(2,1)}) custom-call(bf16[2048,1024]{1,0:T(8,128)(2,1)} %bitcast.4, bf16[4,1024,4096]{2,1,0:T(8,128)(2,1)} %w1_ref.3, bf16[4,4096,1024]{2,1,0:T(8,128)(2,1)} %w2_ref.3), custom_call_target="tpu_custom_call" | custom-call | tf_op jit(solution)/shard_map/forward_stack/pallas_call | solution.py:63
  164.9 175.3 %backward_stack.1 = (bf16[4,2048,1024]{2,1,0:T(8,128)(2,1)}, bf16[4,2048,4096]{2,1,0:T(8,128)(2,1)}) custom-call(s32[2]{0:T(128)} %len_ref.1, bf16[2048,1024]{1,0:T(8,128)(2,1)} %bitcast.5, bf16[4,2048,4096]{2,1,0:T(8,128)(2,1)} %get-tuple-element.10.h_ref, bf16[4,1024,4096]{2,1,0:T(8,128)(2,1)} %w1_ref.3, bf16[4,4096,1024]{2,1,0:T(8,128)(2,1)} %w2_ref.3), custom_call_target="tpu_custom_call" | custom-call | tf_op jit(solution)/shard_map/backward_stack/pallas_call | solution.py:119
  340.3 128.7 %gram_norms.1 = f32[4,2,8,128]{3,2,1,0:T(8,128)} custom-call(bf16[4,2048,1024]{2,1,0:T(8,128)(2,1)} %get-tuple-element.9.x_ref.xs_ref, bf16[4,2048,4096]{2,1,0:T(8,128)(2,1)} %get-tuple-element.11.e_ref, bf16[4,2048,4096]{2,1,0:T(8,128)(2,1)} %get-tuple-element.12.a_ref, bf16[4,2048,1024]{2,1,0:T(8,128)(2,1)} %get-tuple-element.13.d_ref), custom_call_target="tpu_custom_call" | custom-call | tf_op jit(solution)/shard_map/gram_norms/pallas_call | solution.py:166
  469.0 0.9 reduce_sum.9
  469.8 0.5 multiply_minimum_fusion.factor_ref
  470.3 449.7 %grad_sums.1 = (bf16[4,1024,4096]{2,1,0:T(8,128)(2,1)}, bf16[4,4096,1024]{2,1,0:T(8,128)(2,1)}) custom-call(f32[2]{0:T(128)} %multiply_minimum_fusion.factor_ref, bf16[4,2048,1024]{2,1,0:T(8,128)(2,1)} %get-tuple-element.9.x_ref.xs_ref, bf16[4,2048,4096]{2,1,0:T(8,128)(2,1)} %get-tuple-element.12.a_ref, bf16[4,2048,1024]{2,1,0:T(8,128)(2,1)} %get-tuple-element.13.d_ref, ...), custom_call_target="tpu_custom_call" | custom-call | tf_op jit(solution)/shard_map/grad_sums/pallas_call | solution.py:353
  920.0 54.2 %finish.2 = f32[4,1024,4096]{2,1,0:T(8,128)} custom-call(bf16[4,1024,4096]{2,1,0:T(8,128)(2,1)} %get-tuple-element.14.total_ref, f32[4,1024,4096]{2,1,0:T(8,128)} %noise_ref.2), custom_call_target="tpu_custom_call" | custom-call | tf_op jit(solution)/shard_map/finish/pallas_call | solution.py:380
  974.3 54.2 %finish.3 = f32[4,4096,1024]{2,1,0:T(8,128)} custom-call(bf16[4,4096,1024]{2,1,0:T(8,128)(2,1)} %get-tuple-element.15.total_ref, f32[4,4096,1024]{2,1,0:T(8,128)} %noise_ref.3), custom_call_target="tpu_custom_call" | custom-call | tf_op jit(solution)/shard_map/finish/pallas_call | solution.py:380

commit v2 on v1

--- a/solution.py
+++ b/solution.py
@@ -9,7 +9,8 @@
 
 BF16 = jnp.bfloat16
 F32 = jnp.float32
-VMEM_LIMIT = 66_000_000
+VMEM_LIMIT = 67_043_328
+WINDOW = 512
 C0 = 0.7978845608028654
 C1 = 0.044715
 NT = (((1,), (1,)), ((), ()))
@@ -30,102 +31,151 @@
     return pltpu.CompilerParams(vmem_limit_bytes=VMEM_LIMIT, dimension_semantics=("arbitrary",) * dims)
 
 
-def forward_kernel(tm, sub, x_ref, w1_ref, w2_ref, xs_ref, h_ref, a_ref, xcur):
+def forward_kernel(tm, nu, nd, x_ref, *refs):
+    w1 = refs[:nu]; w2 = refs[nu:nu + nd]
+    xs_ref, h_ref, a_out, xcur, abuf, sem = refs[nu + nd:]
     layer, m = pl.program_id(0), pl.program_id(1)
-    last = pl.num_programs(0) - 1
+    layers, nm = pl.num_programs(0), pl.num_programs(1)
+    step = layer * nm + m
+    slot = step % 2
+    other = 1 - slot
+    prev = step - 1
+
+    def a_copy(s):
+        return pltpu.make_async_copy(abuf.at[s % 2], a_out.at[s // nm, pl.ds(pl.multiple_of((s % nm) * tm, tm), tm), :], sem.at[s % 2])
+
+    @pl.when(step >= 2)
+    def _():
+        a_copy(step - 2).wait()
+
+    @pl.when(step >= 1)
+    def _():
+        a_copy(prev).start()
+
     rows = pl.ds(pl.multiple_of(m * tm, tm), tm)
-
-    def up():
-        xs_ref[0] = jnp.where(layer == 0, x_ref[...], xcur[rows, :])
-        for s in range(w1_ref.shape[-1] // sub):
-            cols = slice(s * sub, (s + 1) * sub)
-            h = jnp.dot(xs_ref[0], w1_ref[0, :, cols], preferred_element_type=F32).astype(BF16)
-            h_ref[0, :, cols] = h
-            a_ref[0, :, cols] = gelu_tanh(h.astype(F32)).astype(BF16)
-
-    @pl.when(layer < last)
-    def _():
-        up()
-        for s in range(w2_ref.shape[-1] // sub):
-            cols = slice(s * sub, (s + 1) * sub)
-            branch = jnp.dot(a_ref[0], w2_ref[0, :, cols], preferred_element_type=F32)
-            xcur[rows, cols] = (xs_ref[0, :, cols].astype(F32) + branch).astype(BF16)
-
-    @pl.when(layer == last)
-    def _():
-        up()
-
-
-def forward_stack(x, w1, w2, tm=512, sub=512):
+    prow = pl.ds(pl.multiple_of((prev % nm) * tm, tm), tm)
+
+    @pl.when(layer == 0)
+    def _():
+        xcur[rows, :] = x_ref[...]
+
+    xs_ref[0] = xcur[rows, :]
+    r = nu // nd
+
+    def up(s):
+        c = slice(s * WINDOW, (s + 1) * WINDOW)
+        h_ref[0, :, c] = jnp.dot(xs_ref[0], w1[s][0], preferred_element_type=F32).astype(BF16)
+
+    def act(c0, c1):
+        abuf[slot, :, c0:c1] = gelu_tanh(h_ref[0, :, c0:c1].astype(F32)).astype(BF16)
+
+    def down(s):
+        c = slice(s * WINDOW, (s + 1) * WINDOW)
+        branch = jnp.dot(abuf[other], w2[s][0], preferred_element_type=F32)
+        xcur[prow, c] = (xcur[prow, c].astype(F32) + branch).astype(BF16)
+
+    full = (step >= 1) & (prev < (layers - 1) * nm)
+
+    @pl.when(full)
+    def _():
+        for s in range(nd):
+            for q in range(r): up(s * r + q)
+            down(s)
+            act(s * r * WINDOW, (s + 1) * r * WINDOW)
+
+    @pl.when(jnp.logical_not(full))
+    def _():
+        for s in range(nu):
+            up(s)
+            act(s * WINDOW, (s + 1) * WINDOW)
+
+    @pl.when(step == layers * nm - 1)
+    def _():
+        a_copy(prev).wait()
+        a_copy(step).start()
+        a_copy(step).wait()
+
+def forward_stack(x, w1, w2, tm=512):
     layers, dm, df = w1.shape
     m_rows = x.shape[0]
     nm = m_rows // tm
+    nu, nd = df // WINDOW, dm // WINDOW
+
+    def lag(l, m):
+        return jnp.minimum(jnp.maximum(l * nm + m - 1, 0) // nm, layers - 2)
+
     return pl.pallas_call(
-        functools.partial(forward_kernel, tm, sub),
+        functools.partial(forward_kernel, tm, nu, nd),
         grid=(layers, nm),
-        in_specs=[
-            pl.BlockSpec((tm, dm), lambda l, m: (jnp.where(l == 0, m, nm - 1), 0)),
-            pl.BlockSpec((1, dm, df), lambda l, m: (l, 0, 0)),
-            pl.BlockSpec((1, df, dm), lambda l, m: (jnp.minimum(l, layers - 2), 0, 0)),
-        ],
+        in_specs=[pl.BlockSpec((tm, dm), lambda l, m: (jnp.where(l == 0, m, nm - 1), 0))]
+        + [pl.BlockSpec((1, dm, WINDOW), lambda l, m, s=s: (l, 0, s)) for s in range(nu)]
+        + [pl.BlockSpec((1, df, WINDOW), lambda l, m, s=s: (lag(l, m), 0, s)) for s in range(nd)],
         out_specs=[
             pl.BlockSpec((1, tm, dm), lambda l, m: (l, m, 0)),
             pl.BlockSpec((1, tm, df), lambda l, m: (l, m, 0)),
-            pl.BlockSpec((1, tm, df), lambda l, m: (l, m, 0)),
+            pl.BlockSpec(memory_space=pl.ANY),
         ],
         out_shape=[
             jax.ShapeDtypeStruct((layers, m_rows, dm), BF16),
             jax.ShapeDtypeStruct((layers, m_rows, df), BF16),
             jax.ShapeDtypeStruct((layers, m_rows, df), BF16),
         ],
-        scratch_shapes=[pltpu.VMEM((m_rows, dm), BF16)],
+        scratch_shapes=[pltpu.VMEM((m_rows, dm), BF16), pltpu.VMEM((2, tm, df), BF16), pltpu.SemaphoreType.DMA((2,))],
         compiler_params=params(2),
         name="forward_stack",
-    )(x, w1, w2)
-
-
-def backward_kernel(tm, sub, per, len_ref, d_ref, h_ref, w1_ref, w2_ref, ds_ref, e_ref, dcur):
-    step, m = pl.program_id(0), pl.program_id(1)
+    )(x, *([w1] * nu), *([w2] * nd))
+
+
+def backward_kernel(tm, nu, nd, per, len_ref, d_ref, h_ref, *refs):
+    w1 = refs[:nu]; w2 = refs[nu:nu + nd]
+    ds_ref, e_ref, dcur = refs[nu + nd:]
+    layer, m = pl.program_id(0), pl.program_id(1)
     last = pl.num_programs(0) - 1
     rows = pl.ds(pl.multiple_of(m * tm, tm), tm)
-
-    def to_hidden():
+    dm = nd * WINDOW
+
+    @pl.when(layer == 0)
+    def _():
         limit = len_ref[m // per] - (m % per) * tm
-        keep = lax.broadcasted_iota(jnp.int32, (tm, d_ref.shape[-1]), 0) < limit
-        fresh = jnp.where(keep, d_ref[...].astype(F32), 0.0).astype(BF16)
-        ds_ref[0] = jnp.where(step == 0, fresh, dcur[rows, :])
-        for s in range(w1_ref.shape[-1] // sub):
-            cols = slice(s * sub, (s + 1) * sub)
-            da = lax.dot_general(ds_ref[0], w2_ref[0, cols, :], NT, preferred_element_type=F32)
-            e_ref[0, :, cols] = (da * gelu_tanh_grad(h_ref[0, :, cols].astype(F32))).astype(BF16)
-
-    @pl.when(step < last)
-    def _():
-        to_hidden()
-        for s in range(w2_ref.shape[-1] // sub):
-            cols = slice(s * sub, (s + 1) * sub)
-            back = lax.dot_general(e_ref[0], w1_ref[0, cols, :], NT, preferred_element_type=F32)
-            dcur[rows, cols] = (ds_ref[0, :, cols].astype(F32) + back).astype(BF16)
-
-    @pl.when(step == last)
-    def _():
-        to_hidden()
-
-
-def backward_stack(lengths, d, h, w1, w2, seq, tm=512, sub=512):
+        keep = lax.broadcasted_iota(jnp.int32, (tm, dm), 0) < limit
+        dcur[rows, :] = jnp.where(keep, d_ref[...].astype(F32), 0.0).astype(BF16)
+
+    ds_ref[0] = dcur[rows, :]
+
+    def hidden(s):
+        c = slice(s * WINDOW, (s + 1) * WINDOW)
+        da = sum(lax.dot_general(ds_ref[0, :, k * WINDOW:(k + 1) * WINDOW], w2[k][0, c, :], NT, preferred_element_type=F32) for k in range(nd))
+        e_ref[0, :, c] = (da * gelu_tanh_grad(h_ref[0, :, c].astype(F32))).astype(BF16)
+
+    def back(s):
+        c = slice(s * WINDOW, (s + 1) * WINDOW)
+        v = sum(lax.dot_general(e_ref[0, :, k * WINDOW:(k + 1) * WINDOW], w1[k][0, c, :], NT, preferred_element_type=F32) for k in range(nu))
+        dcur[rows, c] = (ds_ref[0, :, c].astype(F32) + v).astype(BF16)
+
+    @pl.when(layer < last)
+    def _():
+        for s in range(nu): hidden(s)
+        for s in range(nd): back(s)
+
+    @pl.when(layer == last)
+    def _():
+        for s in range(nu): hidden(s)
+
+def backward_stack(lengths, d, h, w1, w2, seq, tm=512):
     layers, dm, df = w1.shape
     m_rows = d.shape[0]
     nm = m_rows // tm
+    nu, nd = df // WINDOW, dm // WINDOW
     return pl.pallas_call(
-        functools.partial(backward_kernel, tm, sub, seq // tm),
+        functools.partial(backward_kernel, tm, nu, nd, seq // tm),
         grid=(layers, nm),
         in_specs=[
             pl.BlockSpec(memory_space=pltpu.SMEM),
             pl.BlockSpec((tm, dm), lambda s, m: (jnp.where(s == 0, m, nm - 1), 0)),
             pl.BlockSpec((1, tm, df), lambda s, m: (layers - 1 - s, m, 0)),
-            pl.BlockSpec((1, dm, df), lambda s, m: (jnp.maximum(layers - 1 - s, 1), 0, 0)),
-            pl.BlockSpec((1, df, dm), lambda s, m: (layers - 1 - s, 0, 0)),
-        ],
+        ]
+        + [pl.BlockSpec((1, dm, WINDOW), lambda s, m, k=k: (jnp.maximum(layers - 1 - s, 1), 0, k)) for k in range(nu)]
+        + [pl.BlockSpec((1, df, WINDOW), lambda s, m, k=k: (layers - 1 - s, 0, k)) for k in range(nd)],
         out_specs=[
             pl.BlockSpec((1, tm, dm), lambda s, m: (layers - 1 - s, m, 0)),
             pl.BlockSpec((1, tm, df), lambda s, m: (layers - 1 - s, m, 0)),
@@ -137,7 +187,7 @@
         scratch_shapes=[pltpu.VMEM((m_rows, dm), BF16)],
         compiler_params=params(2),
         name="backward_stack",
-    )(lengths, d, h, w1, w2)
+    )(lengths, d, h, *([w1] * nu), *([w2] * nd))
 
 
 def fold(v):
@@ -181,11 +231,12 @@
 QUARTERS = 4
 LAG = 3
 STAGES = 8
-
-
-def grad_sum_kernel(seq, n_chunks, factor_ref, xs_ref, a_ref, d_ref, e_ref, tot1_ref, tot2_ref,
-                    lhs, raw, rhs, part, sum1, sum2, sum3, got0, got1, got2, got3, full,
-                    load_sem, out_sem, send_sem, recv_sem):
+NOISE_SLOTS = 9
+
+
+def grad_sum_kernel(seq, n_chunks, scale, factor_ref, xs_ref, a_ref, d_ref, e_ref, noise1_ref, noise2_ref, out1_ref, out2_ref,
+                    lhs, raw, rhs, part, sum1, sum2, sum3, got0, got1, got2, got3, full, final,
+                    load_sem, noise_sem, out_sem, send_sem, recv_sem):
     me = lax.axis_index("data")
     rows_all, width = rhs.shape
     tile = part.shape[1]
@@ -277,12 +328,15 @@
         else:
             full[ag, pl.ds(aligned(core * half + b1 * quarter + b2 * eighth + b3 * piece), piece), :] = value
 
-    def out_copy(n, start):
-        block, layer, which = place(n)
-        ag, row = n % AG_SLOTS, (n % QUARTERS) * tile
-
-        def go(dst):
-            copy = pltpu.make_async_copy(full.at[ag], dst, out_sem.at[n % SLOTS])
+    def final_copy(n, inward, start):
+        _, layer, which = place(n)
+        slot, row = n % NOISE_SLOTS, (n % QUARTERS) * tile
+
+        def go(ref):
+            if inward:
+                copy = pltpu.make_async_copy(ref, final.at[slot], noise_sem.at[slot])
+            else:
+                copy = pltpu.make_async_copy(final.at[slot], ref, out_sem.at[slot])
             if start:
                 copy.start()
             else:
@@ -290,11 +344,18 @@
 
         @pl.when(which < QUARTERS)
         def _():
-            go(tot1_ref.at[layer, pl.ds(aligned(row), tile), pl.ds(pl.multiple_of((which % QUARTERS) * width, width), width)])
+            ref = noise1_ref if inward else out1_ref
+            go(ref.at[layer, pl.ds(aligned(row), tile), pl.ds(pl.multiple_of((which % QUARTERS) * width, width), width)])
 
         @pl.when(which >= QUARTERS)
         def _():
-            go(tot2_ref.at[layer, pl.ds(aligned((which % QUARTERS) * width + row), tile), :])
+            ref = noise2_ref if inward else out2_ref
+            go(ref.at[layer, pl.ds(aligned((which % QUARTERS) * width + row), tile), :])
+
+    def finish(n):
+        final_copy(n, True, False)
+        slot = n % NOISE_SLOTS
+        final[slot] = (full[n % AG_SLOTS].astype(F32) + final[slot]) * scale
 
     def guarded(t, offset, fn):
         n = t - offset
@@ -308,7 +369,7 @@
     done = first + STAGES * LAG
 
     def tick(t, carry):
-        guarded(t, done + LAG, lambda n: out_copy(n, False))
+        guarded(t, done + LAG, lambda n: final_copy(n, False, False))
         for stage in range(STAGES):
             def arrive(n, stage=stage):
                 transfer(n, stage).wait()
@@ -317,7 +378,8 @@
             guarded(t, first + LAG * (stage + 1), arrive)
         for stage in range(STAGES):
             guarded(t, first + LAG * stage, lambda n, stage=stage: transfer(n, stage).start())
-        guarded(t, done, lambda n: out_copy(n, True))
+        guarded(t, done, finish)
+        guarded(t, done - LAG, lambda n: final_copy(n, True, True))
 
         def compute(n):
             block = n // QUARTERS
@@ -335,12 +397,13 @@
             cols = pl.ds(pl.multiple_of((n % QUARTERS) * tile, tile), tile)
             part[n % SLOTS] = lax.dot_general(lhs[block % 2, :, cols], rhs[...], TN, preferred_element_type=F32).astype(BF16)
         guarded(t, 0, compute)
+        guarded(t, done, lambda n: final_copy(n, False, True))
         return carry
 
     lax.fori_loop(0, n_chunks + done + LAG, tick, 0)
 
 
-def grad_sums(factor, xs, a, d, e, seq):
+def grad_sums(factor, xs, a, d, e, noise1, noise2, seq, scale):
     layers, rows, dm = xs.shape
     df = a.shape[-1]
     tile = dm // QUARTERS
@@ -351,41 +414,44 @@
         return pltpu.VMEM(shape, BF16)
 
     return pl.pallas_call(
-        functools.partial(grad_sum_kernel, seq, n_chunks),
-        in_specs=[pl.BlockSpec(memory_space=pltpu.SMEM), hbm, hbm, hbm, hbm],
+        functools.partial(grad_sum_kernel, seq, n_chunks, scale),
+        in_specs=[pl.BlockSpec(memory_space=pltpu.SMEM)] + [hbm] * 6,
         out_specs=[hbm, hbm],
-        out_shape=[jax.ShapeDtypeStruct((layers, dm, df), BF16), jax.ShapeDtypeStruct((layers, df, dm), BF16)],
+        out_shape=[jax.ShapeDtypeStruct((layers, dm, df), F32), jax.ShapeDtypeStruct((layers, df, dm), F32)],
         scratch_shapes=[
             vmem(2, rows, dm), vmem(rows, dm), vmem(rows, dm),
             vmem(SLOTS, tile, dm), vmem(SLOTS, tile // 2, dm), vmem(SLOTS, tile // 4, dm), vmem(SLOTS, tile // 8, dm),
             vmem(SLOTS, tile // 2, dm), vmem(SLOTS, tile // 4, dm), vmem(SLOTS, tile // 8, dm), vmem(SLOTS, tile // 16, dm),
             vmem(AG_SLOTS, tile, dm),
+            pltpu.VMEM((NOISE_SLOTS, tile, dm), F32),
             pltpu.SemaphoreType.DMA((2,)),
-            pltpu.SemaphoreType.DMA((SLOTS,)),
+            pltpu.SemaphoreType.DMA((NOISE_SLOTS,)),
+            pltpu.SemaphoreType.DMA((NOISE_SLOTS,)),
             pltpu.SemaphoreType.DMA((STAGES, SLOTS)),
             pltpu.SemaphoreType.DMA((STAGES, SLOTS)),
         ],
         compiler_params=pltpu.CompilerParams(vmem_limit_bytes=VMEM_LIMIT, collective_id=0, has_side_effects=True),
         name="grad_sums",
-    )(factor, xs, a, d, e)
-
-
-def finish_kernel(scale, total_ref, noise_ref, out_ref):
-    out_ref[...] = (total_ref[...].astype(F32) + noise_ref[...]) * scale
-
-
-def finish(total, noise, scale):
-    layers, rows, cols = noise.shape
+    )(factor, xs, a, d, e, noise1, noise2)
+
+
+def hand_over_kernel(src_ref, dst_ref):
+    dst_ref[...] = src_ref[...]
+
+
+def hand_over(v):
+    layers, rows, cols = v.shape
     tile = (1 << 20) // cols
+    spec = pl.BlockSpec((1, tile, cols), lambda l, r: (l, r, 0))
     return pl.pallas_call(
-        functools.partial(finish_kernel, scale),
+        hand_over_kernel,
         grid=(layers, rows // tile),
-        in_specs=[pl.BlockSpec((1, tile, cols), lambda l, r: (l, r, 0))] * 2,
-        out_specs=pl.BlockSpec((1, tile, cols), lambda l, r: (l, r, 0)),
-        out_shape=jax.ShapeDtypeStruct(noise.shape, F32),
+        in_specs=[spec],
+        out_specs=spec,
+        out_shape=jax.ShapeDtypeStruct(v.shape, v.dtype),
         compiler_params=params(2),
-        name="finish",
-    )(total, noise)
+        name="hand_over",
+    )(v)
 
 
 def solution(mesh):
@@ -398,9 +464,8 @@
         d, e = backward_stack(lengths, dy.reshape(rows, dm), h, w1, w2, seq)
         norms = jnp.sum(gram_norms(xs, e, a, d, seq), axis=(0, 2, 3))
         factor = jnp.minimum(1.0, clip[0] / jnp.sqrt(norms))
-        scale = 1.0 / (samples * devices)
-        total1, total2 = grad_sums(factor, xs, a, d, e, seq)
-        return finish(total1, noise1, scale), finish(total2, noise2, scale)
+        out1, out2 = grad_sums(factor, xs, a, d, e, noise1, noise2, seq, 1.0 / (samples * devices))
+        return hand_over(out1), hand_over(out2)
 
     data, whole = P("data"), P()
     return jax.shard_map(

time: 1040 us -> 1010 us (0.971)
  Pallas kernels: 1030 us -> 992 us
    pallas_call x5, Pallas kernels: 897 us -> 863 us  [the longest x1 451 us: grad_sums(): pl.pallas_call(functools.partial(grad_sum_kernel, seq, n_chunks, scale),...]
where the time goes in v2:
time: 1010 us; the launch traced here: 995 us
  Pallas kernels  992 us (98%)
    pallas_call x1, Pallas kernels, grad_sums(): pl.pallas_call(functools.partial(grad_sum_kernel, seq, n_chunks, scale),...  451 us
    pallas_call x1, Pallas kernels, backward_stack(): pl.pallas_call(functools.partial(backward_kernel, tm, nu, nd, seq // tm),...  175 us
    pallas_call x1, Pallas kernels, forward_stack(): pl.pallas_call(functools.partial(forward_kernel, tm, nu, nd), grid=(layer...  147 us
    pallas_call x1, Pallas kernels, gram_norms(): pl.pallas_call(functools.partial(gram_kernel, bs), grid=(layers, m_rows /...  129 us
    pallas_call x2, Pallas kernels, hand_over(): pl.pallas_call(hand_over_kernel, grid=(layers, rows // tile), in_specs=[s...  89.4 us

profile of v2, /device:TPU:0, one launch (start us, length us, event | category | flops | bytes accessed | tf_op | source)
XLA Modules:
  0.0 995.1 jit_solution(190380063722863903)
XLA Ops:
  1.3 147.2 %forward_stack.1 = (bf16[4,2048,1024]{2,1,0:T(8,128)(2,1)}, bf16[4,2048,4096]{2,1,0:T(8,128)(2,1)}, bf16[4,2048,4096]{2,1,0:T(8,128)(2,1)}) custom-call(bf16[2048,1024]{1,0:T(8,128)(2,1)} %bitcast.5, bf16[4,1024,4096]{2,1,0:T(8,128)(2,1)} %refs_7_.3, bf16[4,1024,4096]{2,1,0:T(8,128)(2,1)} %refs_7_.3, bf16[4,1024,4096]{2,1,0:T(8,128)(2,1)} %refs_7_.3, ...), custom_call_target="tpu_custom_call" | custom-call | tf_op jit(solution)/shard_map/forward_stack/pallas_call | solution.py:107
  148.4 175.3 %backward_stack.1 = (bf16[4,2048,1024]{2,1,0:T(8,128)(2,1)}, bf16[4,2048,4096]{2,1,0:T(8,128)(2,1)}) custom-call(s32[2]{0:T(128)} %len_ref.1, bf16[2048,1024]{1,0:T(8,128)(2,1)} %bitcast.4, bf16[4,2048,4096]{2,1,0:T(8,128)(2,1)} %get-tuple-element.10.h_ref, bf16[4,1024,4096]{2,1,0:T(8,128)(2,1)} %refs_7_.3, bf16[4,1024,4096]{2,1,0:T(8,128)(2,1)} %refs_7_.3, ...), custom_call_target="tpu_custom_call" | custom-call | tf_op jit(solution)/shard_map/backward_stack/pallas_call | solution.py:169
  323.7 128.6 %gram_norms.1 = f32[4,2,8,128]{3,2,1,0:T(8,128)} custom-call(bf16[4,2048,1024]{2,1,0:T(8,128)(2,1)} %get-tuple-element.9.x_ref.xs_ref, bf16[4,2048,4096]{2,1,0:T(8,128)(2,1)} %get-tuple-element.11.e_ref, bf16[4,2048,4096]{2,1,0:T(8,128)(2,1)} %get-tuple-element.12.a_ref, bf16[4,2048,1024]{2,1,0:T(8,128)(2,1)} %get-tuple-element.13.d_ref), custom_call_target="tpu_custom_call" | custom-call | tf_op jit(solution)/shard_map/gram_norms/pallas_call | solution.py:216
  452.4 0.9 reduce_sum.9
  453.2 0.5 multiply_minimum_fusion.factor_ref
  453.7 451.5 %grad_sums.1 = (f32[4,1024,4096]{2,1,0:T(8,128)}, f32[4,4096,1024]{2,1,0:T(8,128)}) custom-call(f32[2]{0:T(128)} %multiply_minimum_fusion.factor_ref, bf16[4,2048,1024]{2,1,0:T(8,128)(2,1)} %get-tuple-element.9.x_ref.xs_ref, bf16[4,2048,4096]{2,1,0:T(8,128)(2,1)} %get-tuple-element.12.a_ref, bf16[4,2048,1024]{2,1,0:T(8,128)(2,1)} %get-tuple-element.13.d_ref, ...), custom_call_target="tpu_custom_call" | custom-call | tf_op jit(solution)/shard_map/grad_sums/pallas_call | solution.py:416
  905.2 44.7 %hand_over.2 = f32[4,1024,4096]{2,1,0:T(8,128)} custom-call(f32[4,1024,4096]{2,1,0:T(8,128)} %get-tuple-element.14.src_ref), custom_call_target="tpu_custom_call" | custom-call | tf_op jit(solution)/shard_map/hand_over/pallas_call | solution.py:446
  949.9 44.7 %hand_over.3 = f32[4,4096,1024]{2,1,0:T(8,128)} custom-call(f32[4,4096,1024]{2,1,0:T(8,128)} %get-tuple-element.15.src_ref), custom_call_target="tpu_custom_call" | custom-call | tf_op jit(solution)/shard_map/hand_over/pallas_call | solution.py:446
